TPU v7x, 32 devices: a whole 2x2x4 slice. The times are simulated.
32 devices in a mesh: dp: 8 (over y, x, core), tensor: 4 (over z).
Axes of the slice: x: 2, y: 2, z: 4, core: 2. Of those that a mesh axis runs over, the one named last changes fastest.
Arguments:
- inputs: bfloat16 [4, 4096, 768], P(None, ('dp', 'tensor')), may hold values from -12 to 12
- cotangent: bfloat16 [4, 4096, 768], P(None, ('dp', 'tensor')), may hold values from -12 to 12
- segment_ids: int32 [4, 8, 512], P(None, 'dp'), may hold values from 0 to 23, never falling along the last dimension, each value on 1 to 48 neighbouring positions
- ln1_gain: float32 [768], replicated, may hold values from 0.25 to 1.75
- ln1_bias: float32 [768], replicated, may hold values from -1.75 to 1.75
- qkv_weight: bfloat16 [3, 768, 768], P(None, 'dp', 'tensor'), may hold values from -0.21875 to 0.21875
- qv_bias: float32 [2, 768], P(None, 'tensor'), may hold values from -1.75 to 1.75
- out_weight: bfloat16 [768, 768], P('tensor', 'dp'), may hold values from -0.4375 to 0.4375
- out_bias: float32 [768], replicated, may hold values from -1.75 to 1.75
- ln2_gain: float32 [768], replicated, may hold values from 0.25 to 1.75
- ln2_bias: float32 [768], replicated, may hold values from -1.75 to 1.75
- up_weight: bfloat16 [768, 3072], P('dp', 'tensor'), may hold values from -0.21875 to 0.21875
- up_bias: float32 [3072], P('tensor'), may hold values from -1.75 to 1.75
- down_weight: bfloat16 [3072, 768], P('tensor', 'dp'), may hold values from -0.109375 to 0.109375
- down_bias: float32 [768], replicated, may hold values from -1.75 to 1.75
Outputs:
- outputs: float32 [4, 4096, 768], P(None, ('dp', 'tensor'))
- input_grad: float32 [4, 4096, 768], P(None, ('dp', 'tensor'))
- ln1_gain_grad: float32 [768], replicated
- ln1_bias_grad: float32 [768], replicated
- qkv_weight_grad: float32 [3, 768, 768], P(None, 'dp', 'tensor')
- qv_bias_grad: float32 [2, 768], replicated
- out_weight_grad: float32 [768, 768], P('tensor', 'dp')
- out_bias_grad: float32 [768], replicated
- ln2_gain_grad: float32 [768], replicated
- ln2_bias_grad: float32 [768], replicated
- up_weight_grad: float32 [768, 3072], P('dp', 'tensor')
- up_bias_grad: float32 [3072], replicated
- down_weight_grad: float32 [3072, 768], P('tensor', 'dp')
- down_bias_grad: float32 [768], replicated
Inputs may be any that keep to these rules, and one draw needn't show every extreme that they name: `segment_ids`: along each sequence of 512 tokens the ids never fall; a caption spans 1 to 48 tokens, and one caption of each sequence exactly 48.
All inputs are finite; a program needn't handle non-finite values.
Results may differ from a plain program's by a relative error of at most 0.017.
Values may be sent and summed in bfloat16 or wider, within the bound.
A program may use at most 192 MiB of HBM per device.

v0:
```python
import jax
import jax.numpy as jnp
from jax import lax
from jax.sharding import PartitionSpec as P

HD = 64


epsilon = 1e-05
masked_value = -1000000000.0


def layer_norm(stream_values, scales, shifts):
    centered = stream_values - jnp.mean(stream_values, -1, keepdims=True)
    variance = jnp.mean(centered * centered, -1, keepdims=True)
    return centered * lax.rsqrt(variance + epsilon) * scales + shifts


def gelu_exact(hidden):
    return jax.nn.gelu(hidden, approximate=False)


def contract(operand_left, operand_right, left_dim, right_dim):
    return lax.dot_general(
        operand_left,
        operand_right,
        (((left_dim,), (right_dim,)), ((), ())),
        preferred_element_type=jnp.float32,
    )


def gather_rows(values_low):
    return lax.all_gather(values_low, "tensor", axis=0, tiled=True)


def gather_grads(values_low):
    return lax.all_gather(values_low, "tensor", axis=0, tiled=True)


def rows_sum(operand_left, operand_right, einsum_form):
    return lax.psum_scatter(
        jnp.einsum(
            einsum_form, operand_left, operand_right, preferred_element_type=jnp.float32
        ).astype(jnp.bfloat16),
        "tensor",
        scatter_dimension=0,
        tiled=True,
    ).astype(jnp.float32)


def grads_sum(operand_left, operand_right, einsum_form):
    return lax.psum_scatter(
        jnp.einsum(
            einsum_form, operand_left, operand_right, preferred_element_type=jnp.float32
        ).astype(jnp.bfloat16),
        "tensor",
        scatter_dimension=0,
        tiled=True,
    ).astype(jnp.float32)


def scores_of(query_heads, key_heads, same_caption):
    raw_scores = jnp.einsum(
        "bqhd,bkhd->bhqk", query_heads, key_heads, preferred_element_type=jnp.float32
    )
    return jnp.where(same_caption, raw_scores * HD ** (-0.5), masked_value)


def body(
    inputs,
    cotangent,
    segment_ids,
    ln1_gain,
    ln1_bias,
    qkv_weight,
    qv_bias,
    out_weight,
    out_bias,
    ln2_gain,
    ln2_bias,
    up_weight,
    up_bias,
    down_weight,
    down_bias,
):
    batches, shard_rows, model_width = inputs.shape
    sequences, seq_length = (segment_ids.shape[1], segment_ids.shape[2])
    head_cols = qkv_weight.shape[2]
    local_heads = head_cols // HD
    hidden_local = up_weight.shape[1]
    full_rows = sequences * seq_length
    shape_heads = (sequences, seq_length, local_heads, HD)
    tensor_pos = lax.axis_index("tensor")
    zero_index = tensor_pos * 0
    full_grads = (
        jnp.zeros((3, model_width, head_cols), jnp.float32),
        jnp.zeros((head_cols, model_width), jnp.float32),
        jnp.zeros((model_width, hidden_local), jnp.float32),
        jnp.zeros((hidden_local, model_width), jnp.float32),
    )
    qv_total = jnp.zeros((2, head_cols), jnp.float32)
    up_total = jnp.zeros((hidden_local,), jnp.float32)
    out_total = jnp.zeros((model_width,), jnp.float32)
    down_total = jnp.zeros((model_width,), jnp.float32)
    gain1_total = jnp.zeros((model_width,), jnp.float32)
    shift1_total = jnp.zeros((model_width,), jnp.float32)
    gain2_total = jnp.zeros((model_width,), jnp.float32)
    shift2_total = jnp.zeros((model_width,), jnp.float32)
    result_list = []
    input_list = []
    for micro_index in range(batches):
        weights_now = (
            lax.all_gather(qkv_weight, "dp", axis=1, tiled=True),
            lax.all_gather(out_weight, "dp", axis=1, tiled=True),
            lax.all_gather(up_weight, "dp", axis=0, tiled=True),
            lax.all_gather(down_weight, "dp", axis=1, tiled=True),
        )
        qkv_full, out_full, up_full, down_full = weights_now
        segment_now = segment_ids[micro_index]
        same_caption = (segment_now[:, :, None] == segment_now[:, None, :])[:, None]
        stream = inputs[micro_index].astype(jnp.float32)
        normed, norm_pull = jax.vjp(layer_norm, stream, ln1_gain, ln1_bias)
        normed_rows = gather_rows(normed.astype(jnp.bfloat16))
        query_heads = (
            (contract(normed_rows, qkv_full[0], 1, 0) + qv_bias[0])
            .astype(jnp.bfloat16)
            .reshape(shape_heads)
        )
        key_heads = (
            contract(normed_rows, qkv_full[1], 1, 0).astype(jnp.bfloat16).reshape(shape_heads)
        )
        value_heads = (
            (contract(normed_rows, qkv_full[2], 1, 0) + qv_bias[1])
            .astype(jnp.bfloat16)
            .reshape(shape_heads)
        )
        scores = scores_of(query_heads, key_heads, same_caption)
        row_top = jnp.max(scores, -1, keepdims=True)
        shifted = jnp.exp(scores - row_top)
        row_total = jnp.sum(shifted, -1, keepdims=True)
        log_total = row_top + jnp.log(row_total)
        probs_low = (shifted / row_total).astype(jnp.bfloat16)
        mixed = jnp.einsum(
            "bhqk,bkhd->bqhd", probs_low, value_heads, preferred_element_type=jnp.float32
        )
        mixed = mixed.reshape(full_rows, head_cols).astype(jnp.bfloat16)
        middle = stream + rows_sum(mixed, out_full, "sc,cd->sd") + out_bias
        normed_two, norm_two_pull = jax.vjp(layer_norm, middle, ln2_gain, ln2_bias)
        normed_two_rows = gather_rows(normed_two.astype(jnp.bfloat16))
        hidden = contract(normed_two_rows, up_full, 1, 0) + up_bias
        active, gelu_pull = jax.vjp(gelu_exact, hidden)
        active_low = active.astype(jnp.bfloat16)
        feed_out = rows_sum(active_low, down_full, "sc,cd->sd") + down_bias
        result_list.append(middle + feed_out)
        grad_stream = cotangent[micro_index].astype(jnp.float32)
        feed_grad = cotangent[micro_index]
        down_total = down_total + jnp.sum(feed_grad.astype(jnp.float32), 0)
        feed_rows = gather_grads(feed_grad)
        grad_down = contract(active_low, feed_rows, 0, 0)
        hidden_grad = gelu_pull(contract(feed_rows, down_full, 1, 1))[0].astype(jnp.bfloat16)
        up_total = up_total + jnp.sum(hidden_grad.astype(jnp.float32), 0)
        grad_up = contract(normed_two_rows, hidden_grad, 0, 0)
        normed_two_grad = grads_sum(hidden_grad, up_full, "sc,dc->sd")
        middle_part, gain2_grad, shift2_grad = norm_two_pull(normed_two_grad)
        gain2_total = gain2_total + gain2_grad
        shift2_total = shift2_total + shift2_grad
        middle_grad = grad_stream + middle_part
        branch_grad = middle_grad.astype(jnp.bfloat16)
        out_total = out_total + jnp.sum(branch_grad.astype(jnp.float32), 0)
        branch_rows = gather_grads(branch_grad)
        grad_out = contract(mixed, branch_rows, 0, 0)
        mixed_grad = contract(branch_rows, out_full, 1, 1).astype(jnp.bfloat16).reshape(shape_heads)
        attention = jnp.exp(scores_of(query_heads, key_heads, same_caption) - log_total)
        probs_grad = jnp.einsum(
            "bqhd,bkhd->bhqk", mixed_grad, value_heads, preferred_element_type=jnp.float32
        )
        value_grad = jnp.einsum(
            "bhqk,bqhd->bkhd",
            attention.astype(jnp.bfloat16),
            mixed_grad,
            preferred_element_type=jnp.float32,
        )
        scores_grad = attention * (probs_grad - jnp.sum(attention * probs_grad, -1, keepdims=True))
        scores_grad = scores_grad.astype(jnp.bfloat16)
        query_grad = jnp.einsum(
            "bhqk,bkhd->bqhd", scores_grad, key_heads, preferred_element_type=jnp.float32
        ) * HD ** (-0.5)
        key_grad = jnp.einsum(
            "bhqk,bqhd->bkhd", scores_grad, query_heads, preferred_element_type=jnp.float32
        ) * HD ** (-0.5)
        grad_project = jnp.stack(
            [
                query_grad.reshape(full_rows, head_cols),
                key_grad.reshape(full_rows, head_cols),
                value_grad.reshape(full_rows, head_cols),
            ],
            1,
        ).astype(jnp.bfloat16)
        qv_total = qv_total + jnp.sum(grad_project[:, 0::2].astype(jnp.float32), 0)
        grad_qkv = jnp.einsum(
            "sd,sjc->jdc", normed_rows, grad_project, preferred_element_type=jnp.float32
        )
        normed_grad = grads_sum(grad_project, qkv_full, "sjc,jdc->sd")
        stream_part, gain1_grad, shift1_grad = norm_pull(normed_grad)
        gain1_total = gain1_total + gain1_grad
        shift1_total = shift1_total + shift1_grad
        input_list.append(middle_grad + stream_part)
        full_grads = jax.tree.map(jnp.add, full_grads, (grad_qkv, grad_out, grad_up, grad_down))
    qkv_share, out_share, up_share, down_share = (
        lax.psum_scatter(full_grads[0], "dp", scatter_dimension=1, tiled=True),
        lax.psum_scatter(full_grads[1], "dp", scatter_dimension=1, tiled=True),
        lax.psum_scatter(full_grads[2], "dp", scatter_dimension=0, tiled=True),
        lax.psum_scatter(full_grads[3], "dp", scatter_dimension=1, tiled=True),
    )
    qv_whole = lax.dynamic_update_slice(
        jnp.zeros((2, model_width), jnp.float32), qv_total, (zero_index, tensor_pos * head_cols)
    )
    up_whole = lax.dynamic_update_slice(
        jnp.zeros((hidden_local * lax.axis_size("tensor"),), jnp.float32),
        up_total,
        (tensor_pos * hidden_local,),
    )
    summed = lax.psum(
        (
            qv_whole,
            up_whole,
            out_total,
            down_total,
            gain1_total,
            shift1_total,
            gain2_total,
            shift2_total,
        ),
        ("dp", "tensor"),
    )
    qv_sum, up_sum, out_sum, down_sum, gain1_sum, shift1_sum, gain2_sum, shift2_sum = summed
    return (
        jnp.stack(result_list),
        jnp.stack(input_list),
        gain1_sum,
        shift1_sum,
        qkv_share,
        qv_sum,
        out_share,
        out_sum,
        gain2_sum,
        shift2_sum,
        up_share,
        up_sum,
        down_share,
        down_sum,
    )


def solution(mesh):
    in_specs = (
        P(None, ("dp", "tensor"), None),
        P(None, ("dp", "tensor"), None),
        P(None, "dp", None),
        P(),
        P(),
        P(None, "dp", "tensor"),
        P(None, "tensor"),
        P("tensor", "dp"),
        P(),
        P(),
        P(),
        P("dp", "tensor"),
        P("tensor"),
        P("tensor", "dp"),
        P(),
    )
    out_specs = (
        P(None, ("dp", "tensor"), None),
        P(None, ("dp", "tensor"), None),
        P(),
        P(),
        P(None, "dp", "tensor"),
        P(),
        P("tensor", "dp"),
        P(),
        P(),
        P(),
        P("dp", "tensor"),
        P(),
        P("tensor", "dp"),
        P(),
    )
    return jax.shard_map(body, mesh=mesh, in_specs=in_specs, out_specs=out_specs, check_vma=False)
```

profile of v0, /device:TPU:0, one launch (start us, length us, event | category | flops | bytes accessed | tf_op | source)
XLA Modules:
  0.0 885.6 jit_solution(6010277338871002044)
XLA Ops:
  11.8 21.3 %all_gather.72 = bf16[512,768]{1,0:T(8,128)(2,1)S(1)} all-gather(bf16[128,768]{1,0:T(8,128)(2,1)S(1)} %fusion.157), channel_id=1, replica_groups=mesh['dp'=8,'tensor'=4] {'tensor'}, dimensions={0}, use_global_device_ids=true | all-gather | bytes 983040 | tf_op jit(solution)/shard_map/all_gather | solution.py:33
  61.0 21.4 %reduce-scatter.25.cloned.1.call-done = bf16[128,768]{1,0:T(8,128)(2,1)} async-done(((bf16[512,768]{1,0:T(8,128)(2,1)}), bf16[128,768]{1,0:T(8,128)(2,1)}) %reduce-scatter.25.cloned.1.call-update) | async-done | bytes 196624 | tf_op jit(solution)/shard_map/reduce_scatter | solution.py:41
  83.8 17.9 %all_gather.80 = bf16[512,768]{1,0:T(8,128)(2,1)S(1)} all-gather(bf16[128,768]{1,0:T(8,128)(2,1)S(1)} %fusion.153), channel_id=1, replica_groups=mesh['dp'=8,'tensor'=4] {'tensor'}, dimensions={0}, use_global_device_ids=true | all-gather | bytes 983040 | tf_op jit(solution)/shard_map/all_gather | solution.py:33
  110.3 27.5 %all-gather.2 = bf16[1,512,768]{2,1,0:T(8,128)(2,1)} all-gather(bf16[1,128,768]{2,1,0:T(8,128)(2,1)S(1)} %get-tuple-element.151), channel_id=4, replica_groups=mesh['dp'=8,'tensor'=4] {'tensor'}, dimensions={1}, use_global_device_ids=true | all-gather | bytes 983040 | tf_op jit(solution)/shard_map/all_gather | solution.py:37
  137.8 18.3 %all-gather = bf16[1,512,768]{2,1,0:T(8,128)(2,1)} all-gather(bf16[1,128,768]{2,1,0:T(8,128)(2,1)S(1)} %get-tuple-element.149), channel_id=2, replica_groups=mesh['dp'=8,'tensor'=4] {'tensor'}, dimensions={1}, use_global_device_ids=true | all-gather | bytes 983040 | tf_op jit(solution)/shard_map/all_gather | solution.py:37
  163.0 19.6 %all_gather.78 = bf16[512,768]{1,0:T(8,128)(2,1)S(1)} all-gather(bf16[128,768]{1,0:T(8,128)(2,1)S(1)} %get-tuple-element.141), channel_id=1, replica_groups=mesh['dp'=8,'tensor'=4] {'tensor'}, dimensions={0}, use_global_device_ids=true | all-gather | bytes 983040 | tf_op jit(solution)/shard_map/all_gather | solution.py:33
  214.2 23.0 %all_gather.75 = bf16[512,768]{1,0:T(8,128)(2,1)S(1)} all-gather(bf16[128,768]{1,0:T(8,128)(2,1)S(1)} %copy-done.129), channel_id=1, replica_groups=mesh['dp'=8,'tensor'=4] {'tensor'}, dimensions={0}, use_global_device_ids=true | all-gather | bytes 983040 | tf_op jit(solution)/shard_map/all_gather | solution.py:33
  253.1 28.1 %all_gather.82 = bf16[512,768]{1,0:T(8,128)(2,1)S(1)} all-gather(bf16[128,768]{1,0:T(8,128)(2,1)S(1)} %copy-done.128), channel_id=1, replica_groups=mesh['dp'=8,'tensor'=4] {'tensor'}, dimensions={0}, use_global_device_ids=true | all-gather | bytes 983040 | tf_op jit(solution)/shard_map/all_gather | solution.py:33
  292.7 22.7 %all-gather.3 = bf16[1,512,768]{2,1,0:T(8,128)(2,1)} all-gather(bf16[1,128,768]{2,1,0:T(8,128)(2,1)S(1)} %copy-done.107), channel_id=5, replica_groups=mesh['dp'=8,'tensor'=4] {'tensor'}, dimensions={1}, use_global_device_ids=true | all-gather | bytes 983040 | tf_op jit(solution)/shard_map/all_gather | solution.py:37
  315.4 24.2 %all-gather.1 = bf16[1,512,768]{2,1,0:T(8,128)(2,1)} all-gather(bf16[1,128,768]{2,1,0:T(8,128)(2,1)S(1)} %copy-done.106), channel_id=3, replica_groups=mesh['dp'=8,'tensor'=4] {'tensor'}, dimensions={1}, use_global_device_ids=true | all-gather | bytes 983040 | tf_op jit(solution)/shard_map/all_gather | solution.py:37
  346.9 20.2 %reduce-scatter.27.cloned.1.call-done = bf16[128,768]{1,0:T(8,128)(2,1)} async-done(((bf16[512,768]{1,0:T(8,128)(2,1)}), bf16[128,768]{1,0:T(8,128)(2,1)}) %reduce-scatter.27.cloned.1.call-update) | async-done | bytes 196624 | tf_op jit(solution)/shard_map/reduce_scatter | solution.py:41
  371.1 27.1 %all_gather.83 = bf16[512,768]{1,0:T(8,128)(2,1)S(1)} all-gather(bf16[128,768]{1,0:T(8,128)(2,1)S(1)} %get-tuple-element.137), channel_id=1, replica_groups=mesh['dp'=8,'tensor'=4] {'tensor'}, dimensions={0}, use_global_device_ids=true | all-gather | bytes 983040 | tf_op jit(solution)/shard_map/all_gather | solution.py:33
  408.4 19.2 %all_gather.79 = bf16[512,768]{1,0:T(8,128)(2,1)} all-gather(bf16[128,768]{1,0:T(8,128)(2,1)} %get-tuple-element.136), channel_id=1, replica_groups=mesh['dp'=8,'tensor'=4] {'tensor'}, dimensions={0}, use_global_device_ids=true | all-gather | bytes 983040 | tf_op jit(solution)/shard_map/all_gather | solution.py:33
  431.7 25.4 %all_gather.89 = bf16[512,768]{1,0:T(8,128)(2,1)S(1)} all-gather(bf16[128,768]{1,0:T(8,128)(2,1)S(1)} %get-tuple-element.109), channel_id=1, replica_groups=mesh['dp'=8,'tensor'=4] {'tensor'}, dimensions={0}, use_global_device_ids=true | all-gather | bytes 983040 | tf_op jit(solution)/shard_map/all_gather | solution.py:37
  491.8 24.8 %reduce-scatter.51.cloned.1.call-done = bf16[128,768]{1,0:T(8,128)(2,1)} async-done(((bf16[512,768]{1,0:T(8,128)(2,1)}), bf16[128,768]{1,0:T(8,128)(2,1)}) %reduce-scatter.51.cloned.1.call-update) | async-done | bytes 196624 | tf_op jit(solution)/shard_map/reduce_scatter | solution.py:52
  519.4 22.0 %reduce-scatter.31.cloned.1.call-done = bf16[128,768]{1,0:T(8,128)(2,1)} async-done(((bf16[512,768]{1,0:T(8,128)(2,1)}), bf16[128,768]{1,0:T(8,128)(2,1)}) %reduce-scatter.31.cloned.1.call-update) | async-done | bytes 196624 | tf_op jit(solution)/shard_map/reduce_scatter | solution.py:41
  543.6 22.8 %reduce-scatter.39.cloned.1.call-done = bf16[128,768]{1,0:T(8,128)(2,1)} async-done(((bf16[512,768]{1,0:T(8,128)(2,1)}), bf16[128,768]{1,0:T(8,128)(2,1)}) %reduce-scatter.39.cloned.1.call-update) | async-done | bytes 196624 | tf_op jit(solution)/shard_map/reduce_scatter | solution.py:41
  569.5 18.2 %all_gather.85 = bf16[512,768]{1,0:T(8,128)(2,1)S(1)} all-gather(bf16[128,768]{1,0:T(8,128)(2,1)S(1)} %get-tuple-element.145), channel_id=1, replica_groups=mesh['dp'=8,'tensor'=4] {'tensor'}, dimensions={0}, use_global_device_ids=true | all-gather | bytes 983040 | tf_op jit(solution)/shard_map/all_gather | solution.py:37
  591.5 17.6 %all_gather.87 = bf16[512,768]{1,0:T(8,128)(2,1)S(1)} all-gather(bf16[128,768]{1,0:T(8,128)(2,1)S(1)} %get-tuple-element.105), channel_id=1, replica_groups=mesh['dp'=8,'tensor'=4] {'tensor'}, dimensions={0}, use_global_device_ids=true | all-gather | bytes 983040 | tf_op jit(solution)/shard_map/all_gather | solution.py:37
  698.1 19.8 %reduce-scatter.47.cloned.1.call-done = bf16[128,768]{1,0:T(8,128)(2,1)} async-done(((bf16[512,768]{1,0:T(8,128)(2,1)}), bf16[128,768]{1,0:T(8,128)(2,1)}) %reduce-scatter.47.cloned.1.call-update) | async-done | bytes 196624 | tf_op jit(solution)/shard_map/reduce_scatter | solution.py:52
  717.9 25.0 %reduce-scatter.55.cloned.1.call-done = bf16[128,768]{1,0:T(8,128)(2,1)} async-done(((bf16[512,768]{1,0:T(8,128)(2,1)}), bf16[128,768]{1,0:T(8,128)(2,1)}) %reduce-scatter.55.cloned.1.call-update) | async-done | bytes 196624 | tf_op jit(solution)/shard_map/reduce_scatter | solution.py:52
  749.7 40.9 %all-reduce = (f32[768]{0:T(1024)}, f32[768]{0:T(1024)}, f32[2,768]{1,0:T(2,128)}, f32[768]{0:T(1024)}, f32[768]{0:T(1024)}, /*index=5*/f32[768]{0:T(1024)}, f32[3072]{0:T(1024)}, f32[768]{0:T(1024)}) all-reduce(f32[768]{0:T(1024)} %add_add_fusion.15, f32[768]{0:T(1024)} %add_add_fusion.14, ...), channel_id=1, replica_groups=mesh['dp'=8,'tensor'=4] {'dp','tensor'}, use_global_device_ids=true, to_apply=%region_64.65 | all-reduce | flops 9216 | bytes 73728 | tf_op jit(solution)/shard_map/psum | solution.py:223
  798.9 32.9 %reduce-scatter.57.cloned.1.call-done = f32[96,768]{1,0:T(8,128)} async-done(((f32[768,768]{1,0:T(8,128)}), f32[96,768]{1,0:T(8,128)}) %reduce-scatter.57.cloned.1.call-update) | async-done | bytes 294928 | tf_op jit(solution)/shard_map/reduce_scatter | solution.py:212
  831.8 46.0 %reduce-scatter.59.cloned.1.call-done = f32[768,96]{0,1:T(8,128)} async-done(((f32[768,768]{0,1:T(8,128)}), f32[768,96]{0,1:T(8,128)}) %reduce-scatter.59.cloned.1.call-update) | async-done | bytes 294928 | tf_op jit(solution)/shard_map/reduce_scatter | solution.py:213
  (717 shorter events, 281.0 us)
Async XLA Ops:
  8.0 74.4 %reduce-scatter.25.cloned.1.call-start = ((), (), s32[]{:S(2)}) async-start(), calls=%async_computation.20 | async-start | bytes 983040 | tf_op jit(solution)/shard_map/reduce_scatter | solution.py:41
  60.8 97.3 %reduce-scatter.33.cloned.1.call-start = ((), (), s32[]{:S(2)}) async-start(), calls=%async_computation.26 | async-start | bytes 983040 | tf_op jit(solution)/shard_map/reduce_scatter | solution.py:41
  108.2 92.2 %all-gather.7.cloned.1.call-start = ((), (), s32[]{:S(2)}) async-start(), calls=%async_computation.21 | async-start | bytes 1327104 | tf_op jit(solution)/shard_map/all_gather | solution.py:115
  108.7 98.4 %all-gather.9.cloned.1.call-start = ((), (), s32[]{:S(2)}) async-start(), calls=%async_computation.22 | async-start | bytes 1327104 | tf_op jit(solution)/shard_map/all_gather | solution.py:116
  109.3 232.6 %reduce-scatter.49.cloned.1.call-start = ((), (), s32[]{:S(2)}) async-start(), calls=%async_computation.34 | async-start | bytes 983040 | tf_op jit(solution)/shard_map/reduce_scatter | solution.py:52
  214.1 127.9 %reduce-scatter.41.cloned.1.call-start = ((), (), s32[]{:S(2)}) async-start(), calls=%async_computation.30 | async-start | bytes 983040 | tf_op jit(solution)/shard_map/reduce_scatter | solution.py:52
  247.9 94.1 %reduce-scatter.29.cloned.1.call-start = ((), (), s32[]{:S(2)}) async-start(), calls=%async_computation.24 | async-start | bytes 983040 | tf_op jit(solution)/shard_map/reduce_scatter | solution.py:41
  282.8 59.2 %reduce-scatter.37.cloned.1.call-start = ((), (), s32[]{:S(2)}) async-start(), calls=%async_computation.28 | async-start | bytes 983040 | tf_op jit(solution)/shard_map/reduce_scatter | solution.py:41
  289.2 77.9 %reduce-scatter.27.cloned.1.call-start = ((), (), s32[]{:S(2)}) async-start(), calls=%async_computation.23 | async-start | bytes 983040 | tf_op jit(solution)/shard_map/reduce_scatter | solution.py:41
  292.5 135.2 %reduce-scatter.35.cloned.1.call-start = ((), (), s32[]{:S(2)}) async-start(), calls=%async_computation.27 | async-start | bytes 983040 | tf_op jit(solution)/shard_map/reduce_scatter | solution.py:41
  341.9 147.2 %reduce-scatter.53.cloned.1.call-start = ((), (), s32[]{:S(2)}) async-start(), calls=%async_computation.36 | async-start | bytes 983040 | tf_op jit(solution)/shard_map/reduce_scatter | solution.py:52
  427.7 64.1 %reduce-scatter.45.cloned.1.call-start = ((), (), s32[]{:S(2)}) async-start(), calls=%async_computation.32 | async-start | bytes 983040 | tf_op jit(solution)/shard_map/reduce_scatter | solution.py:52
  468.8 47.8 %reduce-scatter.51.cloned.1.call-start = ((), (), s32[]{:S(2)}) async-start(), calls=%async_computation.35 | async-start | bytes 983040 | tf_op jit(solution)/shard_map/reduce_scatter | solution.py:52
  477.2 64.2 %reduce-scatter.31.cloned.1.call-start = ((), (), s32[]{:S(2)}) async-start(), calls=%async_computation.25 | async-start | bytes 983040 | tf_op jit(solution)/shard_map/reduce_scatter | solution.py:41
  480.5 85.9 %reduce-scatter.39.cloned.1.call-start = ((), (), s32[]{:S(2)}) async-start(), calls=%async_computation.29 | async-start | bytes 983040 | tf_op jit(solution)/shard_map/reduce_scatter | solution.py:41
  486.5 210.0 %reduce-scatter.63.cloned.1.call-start = ((), (), s32[]{:S(2)}) async-start(), calls=%async_computation.41 | async-start | bytes 884736
  631.2 67.0 %reduce-scatter.43.cloned.1.call-start = ((), (), s32[]{:S(2)}) async-start(), calls=%async_computation.31 | async-start | bytes 983040 | tf_op jit(solution)/shard_map/reduce_scatter | solution.py:52
  638.0 79.9 %reduce-scatter.47.cloned.1.call-start = ((), (), s32[]{:S(2)}) async-start(), calls=%async_computation.33 | async-start | bytes 983040 | tf_op jit(solution)/shard_map/reduce_scatter | solution.py:52
  646.0 96.9 %reduce-scatter.55.cloned.1.call-start = ((), (), s32[]{:S(2)}) async-start(), calls=%async_computation.37 | async-start | bytes 983040 | tf_op jit(solution)/shard_map/reduce_scatter | solution.py:52
  653.9 143.1 %reduce-scatter.61.cloned.1.call-start = ((), (), s32[]{:S(2)}) async-start(), calls=%async_computation.40 | async-start | bytes 2211840
  669.2 162.6 %reduce-scatter.57.cloned.1.call-start = ((), (), s32[]{:S(2)}) async-start(), calls=%async_computation.38 | async-start | bytes 2654208 | tf_op jit(solution)/shard_map/reduce_scatter | solution.py:212
  676.9 201.0 %reduce-scatter.59.cloned.1.call-start = ((), (), s32[]{:S(2)}) async-start(), calls=%async_computation.39 | async-start | bytes 2654208 | tf_op jit(solution)/shard_map/reduce_scatter | solution.py:213
  695.9 97.3 %copy-start.39 = (f32[128,768]{1,0:T(8,128)S(1)}, f32[128,768]{1,0:T(8,128)}, u32[]{:S(2)}) copy-start(f32[128,768]{1,0:T(8,128)} %copy-done.38) | copy-start | bytes 1179652
  695.9 97.3 %copy-start.41 = (f32[128,768]{1,0:T(8,128)S(1)}, f32[128,768]{1,0:T(8,128)}, u32[]{:S(2)}) copy-start(f32[128,768]{1,0:T(8,128)} %copy-done.40) | copy-start | bytes 1179652
  (236 other events, 2655.4 us)
Sparse Core Ops, SparseCore 0:
  60.9 21.5 reduce-scatter.24
  108.3 32.0 reduce-scatter.32
  214.2 30.5 reduce-scatter.48
  248.0 32.9 reduce-scatter.40
  283.2 29.2 reduce-scatter.28
  314.6 26.4 reduce-scatter.36
  343.5 23.5 reduce-scatter.26
  369.4 31.7 reduce-scatter.34
  427.8 29.4 reduce-scatter.52
  468.9 22.8 reduce-scatter.44
  494.1 22.4 reduce-scatter.50
  518.7 22.6 reduce-scatter.30
  543.7 22.6 reduce-scatter.38
Sparse Core Ops, SparseCore 1:
  110.5 23.2 all-gather.6
  135.6 23.8 all-gather.8
  631.3 35.5 reduce-scatter.62
  669.7 23.2 reduce-scatter.42
  695.3 22.6 reduce-scatter.46
  720.2 22.6 reduce-scatter.54
  746.2 39.6 reduce-scatter.60
  789.6 42.1 reduce-scatter.56
  835.6 42.2 reduce-scatter.58
where the time goes:
time: 895 us; the launch traced here: 886 us
  blocking collectives  405 us (45%)
  waiting for transfers between devices  239 us (27%)
  matrix products  116 us (13%)
  other arithmetic  63.9 us (7%)
  local copies, waits for them, and re-layouts  41 us (5%)
  between operations  18.7 us (2%)
    all_gather x8, blocking collectives, gather_rows(): return lax.all_gather(values_low, 'tensor', axis=0, tiled=True)  172 us
    all_gather x8, blocking collectives, gather_grads(): return lax.all_gather(values_low, 'tensor', axis=0, tiled=True)  171 us
    reduce_scatter x8, waiting for transfers between devices, rows_sum(): lax.psum_scatter(jnp.einsum(einsum_form, operand_left, operand_right, pre...  86.4 us
    reduce_scatter x8, waiting for transfers between devices, grads_sum(): lax.psum_scatter(jnp.einsum(einsum_form, operand_left, operand_right, pre...  72.4 us
    dot_general x36, matrix products, contract(): lax.dot_general(operand_left, operand_right, (((left_dim,), (right_dim,))...  56.3 us
    reduce_scatter x1, waiting for transfers between devices, body(): lax.psum_scatter(full_grads[3], 'dp', scatter_dimension=1, tiled=True)  46 us
    psum x1, blocking collectives, body(): lax.psum((qv_whole, up_whole, out_total, down_total, gain1_total, shift1_...  40.9 us
    unnamed x483, local copies, waits for them, and re-layouts  39.4 us
  transfers between devices with their start and end apart: 22, of which 10 were waited for; matrix products, arithmetic and copies ran while one was open for 19% of the time, Pallas kernels for 0%

commit v1 on v0

v1 whole, which is shorter than its diff:
```python
import functools

import jax
import jax.numpy as jnp
from jax import lax
from jax.experimental import pallas as pl
from jax.experimental.pallas import tpu as pltpu
from jax.sharding import PartitionSpec as P

HD = 64
HALO = 48

epsilon = 1e-05
masked_value = -1000000000.0
bf16, f32 = jnp.bfloat16, jnp.float32


def dot(left, right, left_dim, right_dim):
    return lax.dot_general(
        left, right, (((left_dim,), (right_dim,)), ((), ())), preferred_element_type=f32
    )


def norm_stats(values):
    centered = values - jnp.mean(values, -1, keepdims=True)
    rate = lax.rsqrt(jnp.mean(centered * centered, -1, keepdims=True) + epsilon)
    return centered * rate, rate


def norm_back(grad, hat, rate, gain):
    scaled = grad * gain
    return rate * (
        scaled
        - jnp.mean(scaled, -1, keepdims=True)
        - hat * jnp.mean(scaled * hat, -1, keepdims=True)
    )


def head_base(head, heads_shard, head_cols):
    return (head // heads_shard) * 3 * head_cols + (head % heads_shard) * HD


def probs_of(query, key, same):
    scores = jnp.where(same, dot(query, key, 1, 1) * HD ** (-0.5), masked_value)
    shifted = jnp.exp(scores - jnp.max(scores, -1, keepdims=True))
    return shifted / jnp.sum(shifted, -1, keepdims=True)


def attend_kernel(heads, head_cols, rows, column_ref, row_ref, qkv_ref, mixed_ref):
    same = column_ref[0][HALO : HALO + rows] == row_ref[0]
    for head in range(heads):
        base = head_base(head, head_cols // HD, head_cols)
        query = qkv_ref[0, HALO : HALO + rows, base : base + HD]
        key = qkv_ref[0, :, base + head_cols : base + head_cols + HD]
        value = qkv_ref[0, :, base + 2 * head_cols : base + 2 * head_cols + HD]
        probs_low = probs_of(query, key, same).astype(bf16)
        mixed_ref[0, :, head * HD : (head + 1) * HD] = dot(probs_low, value, 1, 0).astype(bf16)


def attend_back_kernel(heads, head_cols, rows, column_ref, row_ref, qkv_ref, grad_ref, out_ref):
    same = column_ref[0] == row_ref[0]
    own = slice(HALO, HALO + rows)
    for head in range(heads):
        base = head_base(head, head_cols // HD, head_cols)
        query = qkv_ref[0, :, base : base + HD]
        key = qkv_ref[0, :, base + head_cols : base + head_cols + HD]
        value = qkv_ref[0, :, base + 2 * head_cols : base + 2 * head_cols + HD]
        grad = grad_ref[0, :, head * HD : (head + 1) * HD]
        probs = probs_of(query, key, same)
        probs_grad = dot(grad, value, 1, 1)
        scores_grad = probs * (probs_grad - jnp.sum(probs * probs_grad, -1, keepdims=True))
        scores_grad = scores_grad.astype(bf16)
        probs_low = probs.astype(bf16)
        query_grad = dot(scores_grad, key, 1, 0) * HD ** (-0.5)
        key_grad = dot(scores_grad, query, 0, 0) * HD ** (-0.5)
        value_grad = dot(probs_low, grad, 0, 0)
        out_ref[0, :, base : base + HD] = query_grad[own].astype(bf16)
        out_ref[0, :, base + head_cols : base + head_cols + HD] = key_grad[own].astype(bf16)
        out_ref[0, :, base + 2 * head_cols : base + 2 * head_cols + HD] = value_grad[own].astype(bf16)


def one_step(*dims):
    return pl.BlockSpec((1,) + dims, lambda step: (step,) + (0,) * len(dims))


def with_halo(own, first_to_left, last_to_right):
    left = lax.ppermute(own[:, -HALO:], "tensor", last_to_right)
    right = lax.ppermute(own[:, :HALO], "tensor", first_to_left)
    return jnp.concatenate([left, own, right], 1)


def body(
    inputs,
    cotangent,
    segment_ids,
    ln1_gain,
    ln1_bias,
    qkv_weight,
    qv_bias,
    out_weight,
    out_bias,
    ln2_gain,
    ln2_bias,
    up_weight,
    up_bias,
    down_weight,
    down_bias,
):
    batches, rows, width = inputs.shape
    assert segment_ids.shape[1] == 1 and rows >= HALO
    shards = lax.axis_size("tensor")
    replicas = lax.axis_size("dp")
    head_cols = qkv_weight.shape[2]
    hidden_cols = up_weight.shape[1]
    heads = shards * head_cols // HD
    depth = up_weight.shape[0]
    place = lax.axis_index("tensor")
    total = batches * rows
    wide = rows + 2 * HALO

    to_left = [(i, i - 1) for i in range(1, shards)]
    to_right = [(i, i + 1) for i in range(shards - 1)]

    def gather(block):
        whole = lax.all_gather(block, ("tensor", "dp"), axis=0, tiled=True)
        return whole.reshape(shards, width, block.shape[1])

    qkv_all = gather(jnp.transpose(qkv_weight, (1, 0, 2)).reshape(depth, 3 * head_cols))
    out_all = gather(out_weight.T)
    up_all = gather(up_weight)
    down_all = gather(down_weight.T)
    biases = lax.all_gather(
        jnp.concatenate([qv_bias[0], jnp.zeros_like(qv_bias[0]), qv_bias[1], up_bias]), "tensor"
    )
    qkv_bias, up_bias_all = biases[:, : 3 * head_cols], biases[:, 3 * head_cols :]

    ids = jnp.pad(segment_ids[:, 0], ((0, 0), (HALO, HALO)), constant_values=-1)
    ids = lax.dynamic_slice(ids, (0, place * rows), (batches, wide))
    id_column, id_row = ids[:, :, None], ids[:, None, :]

    wide_in = with_halo(inputs, to_left, to_right).astype(f32)
    hat_wide, rate_wide = norm_stats(wide_in)
    normed_wide = (hat_wide * ln1_gain + ln1_bias).astype(bf16)
    normed = normed_wide[:, HALO : HALO + rows].reshape(total, width)
    normed_wide = normed_wide.reshape(batches * wide, width)
    qkv = jnp.concatenate(
        [(dot(normed_wide, qkv_all[t], 1, 0) + qkv_bias[t]).astype(bf16) for t in range(shards)], 1
    ).reshape(batches, wide, 3 * width)
    mixed = pl.pallas_call(
        functools.partial(attend_kernel, heads, head_cols, rows),
        grid=(batches,),
        in_specs=[one_step(wide, 1), one_step(1, wide), one_step(wide, 3 * width)],
        out_specs=one_step(rows, width),
        out_shape=jax.ShapeDtypeStruct((batches, rows, width), bf16),
    )(id_column, id_row, qkv).reshape(total, width)

    stream = inputs.astype(f32).reshape(total, width)

    def column(values, t, size):
        return values[:, t * size : (t + 1) * size]

    branch = sum(dot(column(mixed, t, head_cols), out_all[t], 1, 1) for t in range(shards))
    middle = stream + branch + out_bias
    hat_two, rate_two = norm_stats(middle)
    normed_two = (hat_two * ln2_gain + ln2_bias).astype(bf16)
    feed_grad = cotangent.reshape(total, width)
    feed = 0.0
    normed_two_grad = 0.0
    up_grads, down_grads, up_sums = [], [], []
    for t in range(shards):
        hidden = dot(normed_two, up_all[t], 1, 0) + up_bias_all[t]
        cdf = (1 + lax.erf(hidden * 0.5**0.5)) * 0.5
        active = (hidden * cdf).astype(bf16)
        feed = feed + dot(active, down_all[t], 1, 1)
        down_grads.append(dot(feed_grad, active, 0, 0).astype(bf16))
        slope = cdf + hidden * jnp.exp(-0.5 * hidden * hidden) * 0.3989422804014327
        hidden_grad = (dot(feed_grad, down_all[t], 1, 0) * slope).astype(bf16)
        up_sums.append(jnp.sum(hidden_grad.astype(f32), 0))
        up_grads.append(dot(normed_two, hidden_grad, 0, 0).astype(bf16))
        normed_two_grad = normed_two_grad + dot(hidden_grad, up_all[t], 1, 1)
    outputs = middle + feed + down_bias

    middle_grad = feed_grad.astype(f32) + norm_back(normed_two_grad, hat_two, rate_two, ln2_gain)
    branch_grad = middle_grad.astype(bf16)
    branch_wide = with_halo(branch_grad.reshape(batches, rows, width), to_left, to_right)
    branch_wide = branch_wide.reshape(batches * wide, width)
    mixed_grad = jnp.concatenate(
        [dot(branch_wide, out_all[t], 1, 0).astype(bf16) for t in range(shards)], 1
    ).reshape(batches, wide, width)
    out_grads = [
        dot(branch_grad, column(mixed, t, head_cols), 0, 0).astype(bf16) for t in range(shards)
    ]
    qkv_grad = pl.pallas_call(
        functools.partial(attend_back_kernel, heads, head_cols, rows),
        grid=(batches,),
        in_specs=[
            one_step(wide, 1),
            one_step(1, wide),
            one_step(wide, 3 * width),
            one_step(wide, width),
        ],
        out_specs=one_step(rows, 3 * width),
        out_shape=jax.ShapeDtypeStruct((batches, rows, 3 * width), bf16),
    )(id_column, id_row, qkv, mixed_grad).reshape(total, 3 * width)
    qkv_grads = [
        dot(normed, column(qkv_grad, t, 3 * head_cols), 0, 0).astype(bf16) for t in range(shards)
    ]
    normed_grad = sum(
        dot(column(qkv_grad, t, 3 * head_cols), qkv_all[t], 1, 1) for t in range(shards)
    )
    hat = hat_wide[:, HALO : HALO + rows].reshape(total, width)
    rate = rate_wide[:, HALO : HALO + rows].reshape(total, 1)
    input_grad = middle_grad + norm_back(normed_grad, hat, rate, ln1_gain)

    def scatter(blocks):
        parts = jnp.stack([block.reshape(replicas, depth, -1) for block in blocks], 1)
        parts = lax.psum_scatter(parts, "dp", scatter_dimension=0, tiled=True)[0]
        return lax.psum_scatter(parts, "tensor", scatter_dimension=0, tiled=True)[0].astype(f32)

    down_share = scatter(down_grads)
    up_share = scatter(up_grads)
    out_share = scatter(out_grads)
    qkv_share = scatter(qkv_grads)
    qkv_sum = jnp.sum(qkv_grad.astype(f32), 0).reshape(shards, 3, head_cols)
    sums = lax.psum(
        jnp.concatenate(
            [
                qkv_sum[:, 0].reshape(-1),
                qkv_sum[:, 2].reshape(-1),
                *up_sums,
                jnp.sum(branch_grad.astype(f32), 0),
                jnp.sum(feed_grad.astype(f32), 0),
                jnp.sum(normed_grad * hat, 0),
                jnp.sum(normed_grad, 0),
                jnp.sum(normed_two_grad * hat_two, 0),
                jnp.sum(normed_two_grad, 0),
            ]
        ),
        ("dp", "tensor"),
    )
    qv_sum = sums[: 2 * width].reshape(2, width)
    up_sum = sums[2 * width : 2 * width + shards * hidden_cols]
    rest = sums[2 * width + shards * hidden_cols :].reshape(6, width)
    return (
        outputs.reshape(batches, rows, width),
        input_grad.reshape(batches, rows, width),
        rest[2],
        rest[3],
        qkv_share.reshape(depth, 3, head_cols).transpose(1, 0, 2),
        qv_sum,
        out_share.T,
        rest[0],
        rest[4],
        rest[5],
        up_share,
        up_sum,
        down_share.T,
        rest[1],
    )


def solution(mesh):
    in_specs = (
        P(None, ("dp", "tensor"), None),
        P(None, ("dp", "tensor"), None),
        P(None, "dp", None),
        P(),
        P(),
        P(None, "dp", "tensor"),
        P(None, "tensor"),
        P("tensor", "dp"),
        P(),
        P(),
        P(),
        P("dp", "tensor"),
        P("tensor"),
        P("tensor", "dp"),
        P(),
    )
    out_specs = (
        P(None, ("dp", "tensor"), None),
        P(None, ("dp", "tensor"), None),
        P(),
        P(),
        P(None, "dp", "tensor"),
        P(),
        P("tensor", "dp"),
        P(),
        P(),
        P(),
        P("dp", "tensor"),
        P(),
        P("tensor", "dp"),
        P(),
    )
    return jax.shard_map(body, mesh=mesh, in_specs=in_specs, out_specs=out_specs, check_vma=False)
```

time: 895 us -> 665 us (0.74)
  blocking collectives: 405 us -> 58.3 us
  waiting for transfers between devices: 239 us -> 338 us
  Pallas kernels: 0 us -> 50.2 us
  matrix products: 116 us -> 86.4 us
  other arithmetic: 63.9 us -> 38.6 us
  starting transfers between devices: 1.61 us -> 14.4 us
  local copies, waits for them, and re-layouts: 41 us -> 52.2 us
    all_gather x18 -> x0, blocking collectives: 364 us -> none  [the longest x8 172 us: gather_rows(): return lax.all_gather(values_low, 'tensor', axis=0, tiled=True)]
    all_gather x2 -> x4, waiting for transfers between devices: 0.01 us -> 154 us  [gather(): whole = lax.all_gather(block, ('tensor', 'dp'), axis=0, tiled=True)]
    reduce_scatter x18 -> x7, waiting for transfers between devices: 238 us -> 136 us  [the longest x3 96.7 us: scatter(): parts = lax.psum_scatter(parts, 'dp', scatter_dimension=0, tiled=True)[0]]
    pallas_call x0 -> x2, Pallas kernels: none -> 50.2 us  [the longest x1 30.1 us: body(): pl.pallas_call(functools.partial(attend_back_kernel, heads, head_cols, ro...]
    unnamed x24 -> x13, waiting for transfers between devices: 1.39 us -> 48.2 us
    dot_general x80 -> x48, matrix products: 116 us -> 86.4 us  [dot(): lax.dot_general(left, right, (((left_dim,), (right_dim,)), ((), ())), pre...]
    unnamed x483 -> x124, local copies, waits for them, and re-layouts: 39.4 us -> 12.2 us
    reduce_sum x24 -> x6, other arithmetic: 29.2 us -> 3.9 us  [the longest x1 2.22 us: body(): jnp.sum(branch_grad.astype(f32), 0)]
  transfers between devices with their start and end apart: 22 -> 16, of which waited for: 10 -> 9; matrix products, arithmetic and copies ran while one was open for 19% -> 22% of each run, Pallas kernels for 0% -> 8%
where the time goes in v1:
time: 665 us; the launch traced here: 654 us
  waiting for transfers between devices  338 us (51%)
  matrix products  86.4 us (13%)
  blocking collectives  58.3 us (9%)
  local copies, waits for them, and re-layouts  52.2 us (8%)
  Pallas kernels  50.2 us (8%)
  other arithmetic  38.6 us (6%)
  between operations  16.1 us (2%)
  starting transfers between devices  14.4 us (2%)
    all_gather x4, waiting for transfers between devices, gather(): whole = lax.all_gather(block, ('tensor', 'dp'), axis=0, tiled=True)  154 us
    reduce_scatter x3, waiting for transfers between devices, scatter(): parts = lax.psum_scatter(parts, 'dp', scatter_dimension=0, tiled=True)[0]  96.7 us
    dot_general x48, matrix products, dot(): lax.dot_general(left, right, (((left_dim,), (right_dim,)), ((), ())), pre...  86.4 us
    unnamed x13, waiting for transfers between devices  48.2 us
    psum x1, blocking collectives, body(): lax.psum(jnp.concatenate([qkv_sum[:, 0].reshape(-1), qkv_sum[:, 2].reshap...  39.7 us
    reduce_scatter x4, waiting for transfers between devices, scatter(): lax.psum_scatter(parts, 'tensor', scatter_dimension=0, tiled=True)[0]  38.9 us
    pallas_call x1, Pallas kernels, body(): pl.pallas_call(functools.partial(attend_back_kernel, heads, head_cols, ro...  30.1 us
    pallas_call x1, Pallas kernels, body(): pl.pallas_call(functools.partial(attend_kernel, heads, head_cols, rows),...  20.1 us
  transfers between devices with their start and end apart: 16, of which 9 were waited for; matrix products, arithmetic and copies ran while one was open for 22% of the time, Pallas kernels for 8%

profile of v1, /device:TPU:0, one launch (start us, length us, event | category | flops | bytes accessed | tf_op | source)
XLA Modules:
  0.0 654.1 jit_solution(7442335246540500433)
XLA Ops:
  14.6 5.6 collective-permute-start
  23.6 18.6 %all-reduce.1 = f32[5376]{0:T(1024)S(1)} all-reduce(f32[5376]{0:T(1024)S(1)} %dynamic-update-slice), channel_id=2, replica_groups=mesh['dp'=8,'tensor'=4] {'tensor'}, use_global_device_ids=true, to_apply=%add.1 | all-reduce | flops 5376 | bytes 43008
  47.8 27.3 %all-gather.6.cloned.1.call-done = bf16[3072,576]{1,0:T(8,128)(2,1)} async-done(((bf16[96,576]{1,0:T(8,128)(2,1)}), bf16[3072,576]{1,0:T(8,128)(2,1)}) %all-gather.6.cloned.1.call-update) | async-done | bytes 3538960 | tf_op jit(solution)/shard_map/all_gather | solution.py:125
  81.1 9.8 %pad_maximum_fusion.2 = bf16[896,2304]{0,1:T(8,128)(2,1)} fusion(bf16[896,576]{0,1:T(8,128)(2,1)S(1)} %add_convert_fusion, bf16[896,576]{0,1:T(8,128)(2,1)S(1)} %add_convert_fusion.1, bf16[896,576]{0,1:T(8,128)(2,1)S(1)} %add_convert_fusion.2, bf16[896,576]{0,1:T(8,128)(2,1)S(1)} %add_convert_fusion.3), kind=kLoop, calls=%fused_computation.3 | loop fusion | flops 16515072 | bytes 8257536 | tf_op jit(solution)/shard_map/concatenate | solution.py:146
  91.0 6.5 copy.68
  97.5 20.1 %shard_map.254 = bf16[4,128,768]{2,1,0:T(8,128)(2,1)} custom-call(s32[4,224,1]{2,1,0:T(8,128)} %copy.69.column_ref, s32[4,1,224]{2,1,0:T(1,128)} %broadcast_in_dim.7.row_ref, bf16[4,224,2304]{2,1,0:T(8,128)(2,1)} %bitcast.170), custom_call_target="tpu_custom_call" | custom-call | tf_op jit(solution)/shard_map/pallas_call | solution.py:149
  117.6 14.8 %all-gather.8.cloned.1.call-done = bf16[3072,192]{1,0:T(8,128)(2,1)} async-done(((bf16[96,192]{1,0:T(8,128)(2,1)}), bf16[3072,192]{1,0:T(8,128)(2,1)}) %all-gather.8.cloned.1.call-update) | async-done | bytes 1179664 | tf_op jit(solution)/shard_map/all_gather | solution.py:125
  137.9 60.0 %all-gather.10.cloned.1.call-done = bf16[3072,768]{1,0:T(8,128)(2,1)} async-done(((bf16[96,768]{1,0:T(8,128)(2,1)}), bf16[3072,768]{1,0:T(8,128)(2,1)}) %all-gather.10.cloned.1.call-update) | async-done | bytes 4718608 | tf_op jit(solution)/shard_map/all_gather | solution.py:125
  201.1 3.7 multiply_convert_fusion.1
  207.1 3.5 multiply_convert_fusion.2
  210.6 52.0 %all-gather.12.cloned.1.call-done = bf16[3072,768]{1,0:T(8,128)(2,1)} async-done(((bf16[96,768]{1,0:T(8,128)(2,1)}), bf16[3072,768]{1,0:T(8,128)(2,1)}) %all-gather.12.cloned.1.call-update) | async-done | bytes 4718608 | tf_op jit(solution)/shard_map/all_gather | solution.py:125
  262.6 3.6 convert_reduce_fusion.4
  285.9 5.3 collective-permute-start.2
  313.2 30.1 %shard_map.255 = bf16[4,128,2304]{2,1,0:T(8,128)(2,1)} custom-call(s32[4,224,1]{2,1,0:T(8,128)} %copy.69.column_ref, s32[4,1,224]{2,1,0:T(1,128)} %broadcast_in_dim.7.row_ref, bf16[4,224,2304]{2,1,0:T(8,128)(2,1)} %bitcast.171, bf16[4,224,768]{2,1,0:T(8,128)(2,1)} %bitcast.195), custom_call_target="tpu_custom_call" | custom-call | tf_op jit(solution)/shard_map/pallas_call | solution.py:193
  361.4 3.5 pad_maximum_fusion.3
  389.8 3.6 add_add_fusion.2
  394.4 46.8 %all-reduce.5.cloned.1.call-done = bf16[8,4,96,576]{3,2,0,1:T(8,128)(2,1)} async-done(((bf16[8,4,96,576]{3,2,0,1:T(8,128)(2,1)}), bf16[8,4,96,576]{3,2,0,1:T(8,128)(2,1)}) %all-reduce.5.cloned.1.call-update) | async-done | bytes 3538960
  453.6 44.9 %reduce-scatter.15.cloned.1.call-done = bf16[1,4,96,768]{3,2,1,0:T(8,128)(2,1)} async-done(((bf16[8,4,96,768]{3,2,1,0:T(8,128)(2,1)}), bf16[1,4,96,768]{3,2,1,0:T(8,128)(2,1)}) %reduce-scatter.15.cloned.1.call-update) | async-done | bytes 589840 | tf_op jit(solution)/shard_map/reduce_scatter | solution.py:217
  498.6 5.4 fusion.33
  504.1 51.7 %reduce-scatter.19.cloned.1.call-done = bf16[1,4,96,768]{3,2,1,0:T(8,128)(2,1)} async-done(((bf16[8,4,96,768]{3,2,1,0:T(8,128)(2,1)}), bf16[1,4,96,768]{3,2,1,0:T(8,128)(2,1)}) %reduce-scatter.19.cloned.1.call-update) | async-done | bytes 589840 | tf_op jit(solution)/shard_map/reduce_scatter | solution.py:217
  555.8 39.7 %psum.7 = f32[9216]{0:T(1024)S(1)} all-reduce(f32[9216]{0:T(1024)S(1)} %constant_dynamic-update-slice_fusion), channel_id=1, replica_groups=mesh['dp'=8,'tensor'=4] {'dp','tensor'}, use_global_device_ids=true, to_apply=%region_19.20 | all-reduce | flops 9216 | bytes 73728 | tf_op jit(solution)/shard_map/psum | solution.py:225
  597.3 3.9 fusion.32
  604.6 17.8 %reduce-scatter.17.cloned.1.call-done = bf16[1,96,768]{2,1,0:T(8,128)(2,1)} async-done(((bf16[4,96,768]{2,1,0:T(8,128)(2,1)}), bf16[1,96,768]{2,1,0:T(8,128)(2,1)}) %reduce-scatter.17.cloned.1.call-update) | async-done | bytes 147472 | tf_op jit(solution)/shard_map/reduce_scatter | solution.py:218
  624.1 21.1 %reduce-scatter.21.cloned.1.call-done = bf16[1,96,768]{2,1,0:T(8,128)(2,1)} async-done(((bf16[4,96,768]{2,1,0:T(8,128)(2,1)}), bf16[1,96,768]{2,1,0:T(8,128)(2,1)}) %reduce-scatter.21.cloned.1.call-update) | async-done | bytes 147472 | tf_op jit(solution)/shard_map/reduce_scatter | solution.py:218
  (268 shorter events, 138.6 us)
Async XLA Ops:
  7.2 35.3 %copy-start = (bf16[4,128,768]{2,1,0:T(8,128)(2,1)S(1)}, bf16[4,128,768]{2,1,0:T(8,128)(2,1)}, u32[]{:S(2)}) copy-start(bf16[4,128,768]{2,1,0:T(8,128)(2,1)} %param.15) | copy-start | bytes 2359300
  7.2 67.9 %all-gather.6.cloned.1.call-start = ((), (), s32[]{:S(2)}) async-start(), calls=%async_computation.7 | async-start | bytes 4055040 | tf_op jit(solution)/shard_map/all_gather | solution.py:125
  9.2 123.1 %all-gather.8.cloned.1.call-start = ((), (), s32[]{:S(2)}) async-start(), calls=%async_computation.8 | async-start | bytes 1622016 | tf_op jit(solution)/shard_map/all_gather | solution.py:125
  10.8 187.1 %all-gather.10.cloned.1.call-start = ((), (), s32[]{:S(2)}) async-start(), calls=%async_computation.9 | async-start | bytes 4866048 | tf_op jit(solution)/shard_map/all_gather | solution.py:125
  11.6 251.1 %all-gather.12.cloned.1.call-start = ((), (), s32[]{:S(2)}) async-start(), calls=%async_computation.10 | async-start | bytes 4866048 | tf_op jit(solution)/shard_map/all_gather | solution.py:125
  12.1 382.2 %reduce-scatter.11.cloned.1.call-start = ((), (), s32[]{:S(2)}) async-start(), calls=%async_computation.12 | async-start | bytes 1769472 | tf_op jit(solution)/shard_map/reduce_scatter | solution.py:217
  13.3 29.2 %collective-permute-start.1 = (bf16[4,48,768]{2,1,0:T(8,128)(2,1)S(1)}, bf16[4,48,768]{2,1,0:T(8,128)(2,1)S(1)}, u32[]{:S(2)}, u32[]{:S(2)}) collective-permute-start(bf16[4,48,768]{2,1,0:T(8,128)(2,1)S(1)} %get-tuple-element.68), channel_id=1, source_target_pairs={{1,0},{2,1},{3,2},{5,4},{6,5},{7,6},{9,8},{10,9},{11,10},{13,12},{... | collective-permute-start | bytes 884744 | tf_op jit(solution)/shard_map/ppermute | solution.py:88
  14.6 27.9 %collective-permute-start = (bf16[4,48,768]{2,1,0:T(8,128)(2,1)S(1)}, bf16[4,48,768]{2,1,0:T(8,128)(2,1)S(1)}, u32[]{:S(2)}, u32[]{:S(2)}) collective-permute-start(bf16[4,48,768]{2,1,0:T(8,128)(2,1)S(1)} %get-tuple-element.67), channel_id=1, source_target_pairs={{0,1},{1,2},{2,3},{4,5},{5,6},{6,7},{8,9},{9,10},{10,11},{12,13},{... | collective-permute-start | bytes 884744 | tf_op jit(solution)/shard_map/ppermute | solution.py:87
  21.4 22.7 %copy-start.22 = (f32[768]{0:T(1024)S(1)}, f32[768]{0:T(1024)}, u32[]{:S(2)}) copy-start(f32[768]{0:T(1024)} %param.18) | copy-start | bytes 9220
  21.4 22.7 %copy-start.24 = (f32[768]{0:T(1024)S(1)}, f32[768]{0:T(1024)}, u32[]{:S(2)}) copy-start(f32[768]{0:T(1024)} %param.19) | copy-start | bytes 9220
  46.2 29.0 %copy-start.14 = (bf16[896,768]{1,0:T(8,128)(2,1)S(1)}, bf16[896,768]{1,0:T(8,128)(2,1)}, u32[]{:S(2)}) copy-start(bf16[896,768]{1,0:T(8,128)(2,1)} %fusion.3) | copy-start | bytes 4128772
  137.9 66.9 %copy-start.17 = (bf16[512,768]{1,0:T(8,128)(2,1)}, bf16[512,768]{1,0:T(8,128)(2,1)S(1)}, u32[]{:S(2)}) copy-start(bf16[512,768]{1,0:T(8,128)(2,1)S(1)} %add_convert_fusion.5) | copy-start | bytes 2359300
  207.1 55.5 %copy-start.7 = (bf16[4,128,768]{2,1,0:T(8,128)(2,1)S(1)}, bf16[4,128,768]{2,1,0:T(8,128)(2,1)}, u32[]{:S(2)}) copy-start(bf16[4,128,768]{2,1,0:T(8,128)(2,1)} %param.16) | copy-start | bytes 2359300
  284.6 22.8 %collective-permute-start.3 = (bf16[4,48,768]{2,1,0:T(8,128)(2,1)}, bf16[4,48,768]{2,1,0:T(8,128)(2,1)}, u32[]{:S(2)}, u32[]{:S(2)}) collective-permute-start(bf16[4,48,768]{2,1,0:T(8,128)(2,1)} %get-tuple-element.66), channel_id=1, source_target_pairs={{1,0},{2,1},{3,2},{5,4},{6,5},{7,6},{9,8},{10,9},{11,10},{13,12},{... | collective-permute-start | bytes 884744 | tf_op jit(solution)/shard_map/ppermute | solution.py:88
  285.9 21.5 %collective-permute-start.2 = (bf16[4,48,768]{2,1,0:T(8,128)(2,1)}, bf16[4,48,768]{2,1,0:T(8,128)(2,1)}, u32[]{:S(2)}, u32[]{:S(2)}) collective-permute-start(bf16[4,48,768]{2,1,0:T(8,128)(2,1)} %get-tuple-element.65), channel_id=1, source_target_pairs={{0,1},{1,2},{2,3},{4,5},{5,6},{6,7},{8,9},{9,10},{10,11},{12,13},{... | collective-permute-start | bytes 884744 | tf_op jit(solution)/shard_map/ppermute | solution.py:87
  307.3 133.9 %all-reduce.5.cloned.1.call-start = ((), (), s32[]{:S(2)}) async-start(), calls=%async_computation.18 | async-start | bytes 7864320
  313.2 30.1 %copy-start.19 = (bf16[4,128,768]{2,1,0:T(8,128)(2,1)S(1)}, bf16[4,128,768]{2,1,0:T(8,128)(2,1)}, u32[]{:S(2)}) copy-start(bf16[4,128,768]{2,1,0:T(8,128)(2,1)} %get-tuple-element.63) | copy-start | bytes 2359300
  364.9 133.7 %reduce-scatter.15.cloned.1.call-start = ((), (), s32[]{:S(2)}) async-start(), calls=%async_computation.14 | async-start | bytes 5308416 | tf_op jit(solution)/shard_map/reduce_scatter | solution.py:217
  373.1 182.7 %reduce-scatter.19.cloned.1.call-start = ((), (), s32[]{:S(2)}) async-start(), calls=%async_computation.16 | async-start | bytes 5308416 | tf_op jit(solution)/shard_map/reduce_scatter | solution.py:217
  381.7 219.6 %reduce-scatter.13.cloned.1.call-start = ((), (), s32[]{:S(2)}) async-start(), calls=%async_computation.13 | async-start | bytes 245760 | tf_op jit(solution)/shard_map/reduce_scatter | solution.py:218
  393.5 50.6 %copy-start.2 = (bf16[4,128,2304]{2,1,0:T(8,128)(2,1)S(1)}, bf16[4,128,2304]{2,1,0:T(8,128)(2,1)}, u32[]{:S(2)}) copy-start(bf16[4,128,2304]{2,1,0:T(8,128)(2,1)} %shard_map.255) | copy-start | bytes 7077892
  394.3 208.4 %reduce-scatter.9.cloned.1.call-start = ((), (), s32[]{:S(2)}) async-start(), calls=%async_computation.11 | async-start | bytes 614400 | tf_op jit(solution)/shard_map/reduce_scatter | solution.py:218
  443.8 178.7 %reduce-scatter.17.cloned.1.call-start = ((), (), s32[]{:S(2)}) async-start(), calls=%async_computation.15 | async-start | bytes 737280 | tf_op jit(solution)/shard_map/reduce_scatter | solution.py:218
  498.6 146.6 %reduce-scatter.21.cloned.1.call-start = ((), (), s32[]{:S(2)}) async-start(), calls=%async_computation.17 | async-start | bytes 737280 | tf_op jit(solution)/shard_map/reduce_scatter | solution.py:218
  (45 other events, 153.8 us)
Sparse Core Ops, SparseCore 0:
  11.5 63.6 all-gather.5
  78.6 53.6 all-gather.7
  135.2 62.5 all-gather.9
  200.6 61.9 all-gather.11
  307.4 36.6 reduce-scatter.10
  365.0 76.1 all-reduce.4
  444.7 53.8 reduce-scatter.14
  502.0 53.7 reduce-scatter.18
  558.0 19.6 reduce-scatter.12
  579.9 19.8 reduce-scatter.8
  602.1 20.3 reduce-scatter.16
  624.6 20.5 reduce-scatter.20
